TPU v7x, 32 devices: a whole 2x2x4 slice. The times are simulated.
32 devices in a mesh: row: 8 (over y, x, core), col: 4 (over z).
Axes of the slice: x: 2, y: 2, z: 4, core: 2. Of those that a mesh axis runs over, the one named last changes fastest.
Arguments:
- field: float32 [64, 128, 512], P(None, 'row', 'col'), may hold values from -4 to 6.5, as said below
- conductivity: float32 [64, 128, 512], P(None, 'row', 'col'), may hold values from 35 to 5600, as said below
Outputs:
- new_field: float32 [64, 128, 512], P(None, 'row', 'col')
Inputs may be any that keep to these rules, and one draw needn't show every extreme that they name: `field`: finite values. `conductivity`: positive in every cell.
All inputs are finite; a program needn't handle non-finite values.
Results may differ from a plain program's by a relative error of at most 0.0003.
Values sent between devices are 32-bit elements; how exact they have to be, the bound alone decides.
A program may use at most 64 MiB of HBM per device.

v0:
```python
import jax
import jax.numpy as jnp
from jax import lax
from jax.sharding import PartitionSpec as P

z_weight = 0.02


def padded_2(block, sides, width):
    for axis, dim in sides:
        count = lax.axis_size(axis)
        forward = [(i, i + 1) for i in range(count - 1)]
        backward = [(target, source) for source, target in forward]
        low = lax.ppermute(
            lax.slice_in_dim(block, block.shape[dim] - width, None, axis=dim), axis, forward
        )
        high = lax.ppermute(lax.slice_in_dim(block, 0, width, axis=dim), axis, backward)
        block = jnp.concatenate([low, block, high], axis=dim)
    return block


def neighbour(values, line_axis, offset):
    length = values.shape[line_axis]
    widths = [(0, 0)] * values.ndim
    widths[line_axis] = (1, 1)
    padded = jnp.pad(values, widths)
    return lax.slice_in_dim(padded, 1 + offset, 1 + offset + length, axis=line_axis)


def shifted(values, line_axis, stride, fill):
    length = values.shape[line_axis]
    pad_shape = list(values.shape)
    pad_shape[line_axis] = abs(stride)
    padding = jnp.full(pad_shape, fill, values.dtype)
    if stride > 0:
        kept_part = lax.slice_in_dim(values, 0, length - stride, axis=line_axis)
        return jnp.concatenate((padding, kept_part), axis=line_axis)
    kept_part = lax.slice_in_dim(values, -stride, length, axis=line_axis)
    return jnp.concatenate((kept_part, padding), axis=line_axis)


def reduce_lines(below_diag, diagonal, above_diag, columns, line_axis):
    length = diagonal.shape[line_axis]
    stride = 1
    while stride < length:
        left_factor = -below_diag / shifted(diagonal, line_axis, stride, 1.0)
        right_factor = -above_diag / shifted(diagonal, line_axis, -stride, 1.0)
        new_diag = (
            diagonal
            + left_factor * shifted(above_diag, line_axis, stride, 0.0)
            + right_factor * shifted(below_diag, line_axis, -stride, 0.0)
        )
        new_below = left_factor * shifted(below_diag, line_axis, stride, 0.0)
        new_above = right_factor * shifted(above_diag, line_axis, -stride, 0.0)
        columns = [
            column
            + left_factor * shifted(column, line_axis, stride, 0.0)
            + right_factor * shifted(column, line_axis, -stride, 0.0)
            for column in columns
        ]
        below_diag, diagonal, above_diag = (new_below, new_diag, new_above)
        stride = stride * 2
    return (diagonal, columns)


def local_spikes(below_diag, above_diag, right_side, line_axis):
    length = right_side.shape[line_axis]
    position = lax.broadcasted_iota(jnp.int32, right_side.shape, line_axis)
    first_row = position == 0
    last_row = position == length - 1
    diagonal = 1.0 - below_diag - above_diag
    left_column = jnp.where(first_row, below_diag, 0.0)
    right_column = jnp.where(last_row, above_diag, 0.0)
    below_inner = jnp.where(first_row, 0.0, below_diag)
    above_inner = jnp.where(last_row, 0.0, above_diag)
    diagonal, columns = reduce_lines(
        below_inner, diagonal, above_inner, [right_side, left_column, right_column], line_axis
    )
    local_part = columns[0] / diagonal
    left_spike = columns[1] / diagonal
    right_spike = columns[2] / diagonal
    planes = []
    for member in (local_part, left_spike, right_spike):
        planes.append(lax.index_in_dim(member, 0, line_axis, keepdims=False))
        planes.append(lax.index_in_dim(member, length - 1, line_axis, keepdims=False))
    return (local_part, left_spike, right_spike, jnp.stack(planes)[None])


def join_spikes(gathered, local_part, left_spike, right_spike, line_axis, index_here, group_size):
    columns_in = tuple((gathered[:, member] for member in range(6)))
    zero_plane = jnp.zeros_like(columns_in[0][0])

    def forward(state_now, inputs):
        spike_prev, carry_prev = state_now
        head_local, tail_local, head_left, tail_left, head_right, tail_right = inputs
        pivot_here = 1.0 - head_left * spike_prev
        ratio_here = head_right / pivot_here
        first_here = (head_local - head_left * carry_prev) / pivot_here
        spike_next = tail_right + tail_left * spike_prev * ratio_here
        carry_next = tail_local - tail_left * carry_prev + tail_left * spike_prev * first_here
        return ((spike_next, carry_next), (ratio_here, spike_next, first_here, carry_next))

    unused, outputs = lax.scan(forward, (zero_plane, zero_plane), columns_in)

    def backward(next_head, inputs):
        ratio_here, spike_here, first_here, last_here = inputs
        head_value = first_here - ratio_here * next_head
        tail_value = last_here - spike_here * next_head
        return (head_value, (head_value, tail_value))

    unused_last, ends = lax.scan(backward, zero_plane, outputs, reverse=True)
    first_values, last_values = ends
    left_value = lax.dynamic_index_in_dim(
        last_values, jnp.maximum(index_here - 1, 0), 0, keepdims=False
    ) * (index_here > 0).astype(jnp.float32)
    right_value = lax.dynamic_index_in_dim(
        first_values, jnp.minimum(index_here + 1, group_size - 1), 0, keepdims=False
    ) * (index_here < group_size - 1).astype(jnp.float32)
    return (
        local_part
        - jnp.expand_dims(left_value, line_axis) * left_spike
        - jnp.expand_dims(right_value, line_axis) * right_spike
    )


def on_device(field, conductivity):
    stacked = jnp.stack((field, conductivity))
    padded = padded_2(stacked, (("row", 2), ("col", 3)), 1)
    field_pad = padded[0]
    cond_pad = padded[1]
    west_cond = cond_pad[:, :-2, 1:-1]
    east_cond = cond_pad[:, 2:, 1:-1]
    south_cond = cond_pad[:, 1:-1, :-2]
    north_cond = cond_pad[:, 1:-1, 2:]
    west_field = field_pad[:, :-2, 1:-1]
    east_field = field_pad[:, 2:, 1:-1]
    south_field = field_pad[:, 1:-1, :-2]
    north_field = field_pad[:, 1:-1, 2:]
    east_xdir = 0.5 * 1.0 * (conductivity + east_cond)
    west_xdir = 0.5 * 1.0 * (conductivity + west_cond)
    east_ydir = 0.5 * 1.0 * (conductivity + north_cond)
    west_ydir = 0.5 * 1.0 * (conductivity + south_cond)
    flux_xdir = east_xdir * (east_field - field) - west_xdir * (field - west_field)
    flux_ydir = east_ydir * (north_field - field) - west_ydir * (field - south_field)
    east_zdir = 0.5 * z_weight * (conductivity + neighbour(conductivity, 0, 1))
    west_zdir = 0.5 * z_weight * (conductivity + neighbour(conductivity, 0, -1))
    flux_zdir = east_zdir * (neighbour(field, 0, 1) - field) - west_zdir * (
        field - neighbour(field, 0, -1)
    )
    explicit = flux_xdir + flux_ydir + flux_zdir
    local_part, left_spike, right_spike, planes = local_spikes(-west_xdir, -east_xdir, explicit, 1)
    gathered = lax.all_gather(planes, "row", axis=0, tiled=True)
    delta_xdir = join_spikes(
        gathered,
        local_part,
        left_spike,
        right_spike,
        1,
        lax.axis_index("row"),
        lax.axis_size("row"),
    )
    local_part, left_spike, right_spike, planes = local_spikes(
        -west_ydir, -east_ydir, delta_xdir, 2
    )
    gathered = lax.all_gather(planes, "col", axis=0, tiled=True)
    delta_ydir = join_spikes(
        gathered,
        local_part,
        left_spike,
        right_spike,
        2,
        lax.axis_index("col"),
        lax.axis_size("col"),
    )
    return field + delta_ydir


def solution(mesh):
    in_specs = (P(None, "row", "col"), P(None, "row", "col"))
    out_specs = P(None, "row", "col")
    return jax.shard_map(
        on_device, mesh=mesh, in_specs=in_specs, out_specs=out_specs, check_vma=False
    )
```

profile of v0, /device:TPU:0, one launch (start us, length us, event | category | flops | bytes accessed | tf_op | source)
XLA Modules:
  0.0 144.2 jit_solution(15308119017377806291)
XLA Ops:
  6.5 2.5 %fusion.59 = (f32[64,16,128]{2,0,1:T(8,128)}, f32[1,64,16,128]{3,1,2,0:T(8,128)S(1)}, f32[1,64,16,128]{3,1,2,0:T(8,128)S(1)}, f32[64,16,128]{2,0,1:T(8,128)}) fusion(f32[64,16,128]{2,1,0:T(8,128)} %param.10, f32[64,16,128]{2,1,0:T(8,128)} %param.11), kind=kLoop, calls=%fused_computation.241 | loop fusion | bytes 3145728 | tf_op args[0]
  10.4 3.0 %collective-permute-start = (f32[2,64,1,128]{3,1,2,0:T(8,128)S(1)}, f32[2,64,1,128]{3,1,2,0:T(8,128)S(1)}, u32[]{:S(2)}, u32[]{:S(2)}) collective-permute-start(f32[2,64,1,128]{3,1,2,0:T(8,128)S(1)} %get-tuple-element.850), channel_id=1, source_target_pairs={{0,4},{4,8},{8,12},{12,16},{16,20},{20,24},{24,28},{1,5},{5,9},{9,... | collective-permute-start | bytes 196616 | tf_op jit(solution)/shard_map/ppermute | solution.py:14
  17.6 6.2 %collective-permute-start.2 = (f32[2,64,18,1]{1,0,3,2:T(2,128)S(1)}, f32[2,64,18,1]{1,0,3,2:T(2,128)}, u32[]{:S(2)}, u32[]{:S(2)}) collective-permute-start(f32[2,64,18,1]{1,0,3,2:T(2,128)S(1)} %copy.303), channel_id=1, source_target_pairs={{0,1},{1,2},{2,3},{4,5},{5,6},{6,7},{8,9},{9,10},{10,11},{12,13},{... | collective-permute-start | bytes 27656 | tf_op jit(solution)/shard_map/ppermute | solution.py:14
  45.8 23.3 %all-gather.4.cloned.1.call-done = f32[48,64,128]{2,1,0:T(8,128)} async-done(((f32[6,64,128]{2,1,0:T(8,128)}), f32[48,64,128]{2,1,0:T(8,128)}) %all-gather.4.cloned.1.call-update) | async-done | bytes 1572880 | tf_op jit(solution)/shard_map/all_gather | solution.py:152
  69.1 2.4 %slice_bitcast_fusion.2 = (f32[8,64,128]{2,1,0:T(8,128)S(1)}, f32[8,64,128]{2,1,0:T(8,128)S(1)}, f32[8,64,128]{2,1,0:T(8,128)}, f32[8,64,128]{2,1,0:T(8,128)}, f32[8,64,128]{2,1,0:T(8,128)}, /*index=5*/f32[8,64,128]{2,1,0:T(8,128)}) fusion(f32[8,6,64,128]{3,2,1,0:T(8,128)} %bitcast.281), kind=kLoop, calls=%fused_computation.177 | loop fusion | bytes 3145728 | tf_op jit(solution)/shard_map/squeeze | solution.py:90
  74.4 12.1 %while.80 = (s32[]{:T(128)}, f32[64,128]{1,0:T(8,128)S(1)}, f32[64,128]{1,0:T(8,128)S(1)}, f32[8,64,128]{2,1,0:T(8,128)}, f32[8,64,128]{2,1,0:T(8,128)}, /*index...) while((s32[]{:T(128)}, f32[64,128]{1,0:T(8,128)S(1)}, ...), condition=%wide.region_1.2_spmd.clone, body=%wide.region_0.1_spmd.clone.sunk | while | flops 122883 | bytes 458915 | solution.py:103
  74.4 1.6 %bitcast_dynamic-update-slice_fusion.16 = (f32[8,64,128]{2,1,0:T(8,128)}, f32[64,128]{1,0:T(8,128)S(1)}, f32[8,64,128]{2,1,0:T(8,128)}, f32[8,64,128]{2,1,0:T(8,...) fusion(f32[8,64,128]{2,1,0:T(8,128)} %get-tuple-element.1309, s32[]{:T(128)S(6)} %copy.408, ...), kind=kLoop, calls=%fused_computation.clone.1 | loop fusion | flops 122880 | bytes 458757 | tf_op jit(solution)/shard_map/while/body/jit(dynamic_update_index_in_dim)/dynamic_update_slice | solution.py:103
  76.0 1.5 %bitcast_dynamic-update-slice_fusion.16 = (f32[8,64,128]{2,1,0:T(8,128)}, f32[64,128]{1,0:T(8,128)S(1)}, f32[8,64,128]{2,1,0:T(8,128)}, f32[8,64,128]{2,1,0:T(8,...) fusion(f32[8,64,128]{2,1,0:T(8,128)} %get-tuple-element.1309, s32[]{:T(128)S(6)} %copy.408, ...), kind=kLoop, calls=%fused_computation.clone.1 | loop fusion | flops 122880 | bytes 458757 | tf_op jit(solution)/shard_map/while/body/jit(dynamic_update_index_in_dim)/dynamic_update_slice | solution.py:103
  77.5 1.5 %bitcast_dynamic-update-slice_fusion.16 = (f32[8,64,128]{2,1,0:T(8,128)}, f32[64,128]{1,0:T(8,128)S(1)}, f32[8,64,128]{2,1,0:T(8,128)}, f32[8,64,128]{2,1,0:T(8,...) fusion(f32[8,64,128]{2,1,0:T(8,128)} %get-tuple-element.1309, s32[]{:T(128)S(6)} %copy.408, ...), kind=kLoop, calls=%fused_computation.clone.1 | loop fusion | flops 122880 | bytes 458757 | tf_op jit(solution)/shard_map/while/body/jit(dynamic_update_index_in_dim)/dynamic_update_slice | solution.py:103
  79.0 1.5 %bitcast_dynamic-update-slice_fusion.16 = (f32[8,64,128]{2,1,0:T(8,128)}, f32[64,128]{1,0:T(8,128)S(1)}, f32[8,64,128]{2,1,0:T(8,128)}, f32[8,64,128]{2,1,0:T(8,...) fusion(f32[8,64,128]{2,1,0:T(8,128)} %get-tuple-element.1309, s32[]{:T(128)S(6)} %copy.408, ...), kind=kLoop, calls=%fused_computation.clone.1 | loop fusion | flops 122880 | bytes 458757 | tf_op jit(solution)/shard_map/while/body/jit(dynamic_update_index_in_dim)/dynamic_update_slice | solution.py:103
  80.5 1.5 %bitcast_dynamic-update-slice_fusion.16 = (f32[8,64,128]{2,1,0:T(8,128)}, f32[64,128]{1,0:T(8,128)S(1)}, f32[8,64,128]{2,1,0:T(8,128)}, f32[8,64,128]{2,1,0:T(8,...) fusion(f32[8,64,128]{2,1,0:T(8,128)} %get-tuple-element.1309, s32[]{:T(128)S(6)} %copy.408, ...), kind=kLoop, calls=%fused_computation.clone.1 | loop fusion | flops 122880 | bytes 458757 | tf_op jit(solution)/shard_map/while/body/jit(dynamic_update_index_in_dim)/dynamic_update_slice | solution.py:103
  82.0 1.5 %bitcast_dynamic-update-slice_fusion.16 = (f32[8,64,128]{2,1,0:T(8,128)}, f32[64,128]{1,0:T(8,128)S(1)}, f32[8,64,128]{2,1,0:T(8,128)}, f32[8,64,128]{2,1,0:T(8,...) fusion(f32[8,64,128]{2,1,0:T(8,128)} %get-tuple-element.1309, s32[]{:T(128)S(6)} %copy.408, ...), kind=kLoop, calls=%fused_computation.clone.1 | loop fusion | flops 122880 | bytes 458757 | tf_op jit(solution)/shard_map/while/body/jit(dynamic_update_index_in_dim)/dynamic_update_slice | solution.py:103
  83.5 1.5 %bitcast_dynamic-update-slice_fusion.16 = (f32[8,64,128]{2,1,0:T(8,128)}, f32[64,128]{1,0:T(8,128)S(1)}, f32[8,64,128]{2,1,0:T(8,128)}, f32[8,64,128]{2,1,0:T(8,...) fusion(f32[8,64,128]{2,1,0:T(8,128)} %get-tuple-element.1309, s32[]{:T(128)S(6)} %copy.408, ...), kind=kLoop, calls=%fused_computation.clone.1 | loop fusion | flops 122880 | bytes 458757 | tf_op jit(solution)/shard_map/while/body/jit(dynamic_update_index_in_dim)/dynamic_update_slice | solution.py:103
  85.0 1.5 %bitcast_dynamic-update-slice_fusion.16 = (f32[8,64,128]{2,1,0:T(8,128)}, f32[64,128]{1,0:T(8,128)S(1)}, f32[8,64,128]{2,1,0:T(8,128)}, f32[8,64,128]{2,1,0:T(8,...) fusion(f32[8,64,128]{2,1,0:T(8,128)} %get-tuple-element.1309, s32[]{:T(128)S(6)} %copy.408, ...), kind=kLoop, calls=%fused_computation.clone.1 | loop fusion | flops 122880 | bytes 458757 | tf_op jit(solution)/shard_map/while/body/jit(dynamic_update_index_in_dim)/dynamic_update_slice | solution.py:103
  87.9 11.6 %while.81 = (s32[]{:T(128)}, f32[64,128]{1,0:T(8,128)S(1)}, f32[8,64,128]{2,1,0:T(8,128)}, f32[8,64,128]{2,1,0:T(8,128)}, f32[8,64,128]{2,1,0:T(8,128)}, /*index...) while((s32[]{:T(128)}, f32[64,128]{1,0:T(8,128)S(1)}, ...), condition=%wide.region_3.4_spmd.clone, body=%wide.region_2.3_spmd.clone.sunk | while | flops 40964 | bytes 262287 | solution.py:111
  87.9 1.5 %bitcast_dynamic-update-slice_fusion.17 = (f32[8,64,128]{2,1,0:T(8,128)}, f32[64,128]{1,0:T(8,128)S(1)}, f32[8,64,128]{2,1,0:T(8,128)}) fusion(f32[8,64,128]{2,1,0:T(8,128)} %get-tuple-element.1346, s32[]{:T(128)S(6)} %sub.273, f32[64,128]{1,0:T(8,128)S(1)} %get-tuple-element.1345, pred[]{:T(512)S(6)} %compare.143, ...), kind=kLoop, calls=%fused_computation.18.clone.1 | loop fusion | flops 40960 | bytes 262149 | tf_op jit(solution)/shard_map/while/body/jit(dynamic_update_index_in_dim)/dynamic_update_slice | solution.py:103
  90.8 1.5 %bitcast_dynamic-update-slice_fusion.17 = (f32[8,64,128]{2,1,0:T(8,128)}, f32[64,128]{1,0:T(8,128)S(1)}, f32[8,64,128]{2,1,0:T(8,128)}) fusion(f32[8,64,128]{2,1,0:T(8,128)} %get-tuple-element.1346, s32[]{:T(128)S(6)} %sub.273, f32[64,128]{1,0:T(8,128)S(1)} %get-tuple-element.1345, pred[]{:T(512)S(6)} %compare.143, ...), kind=kLoop, calls=%fused_computation.18.clone.1 | loop fusion | flops 40960 | bytes 262149 | tf_op jit(solution)/shard_map/while/body/jit(dynamic_update_index_in_dim)/dynamic_update_slice | solution.py:103
  92.3 1.4 %bitcast_dynamic-update-slice_fusion.17 = (f32[8,64,128]{2,1,0:T(8,128)}, f32[64,128]{1,0:T(8,128)S(1)}, f32[8,64,128]{2,1,0:T(8,128)}) fusion(f32[8,64,128]{2,1,0:T(8,128)} %get-tuple-element.1346, s32[]{:T(128)S(6)} %sub.273, f32[64,128]{1,0:T(8,128)S(1)} %get-tuple-element.1345, pred[]{:T(512)S(6)} %compare.143, ...), kind=kLoop, calls=%fused_computation.18.clone.1 | loop fusion | flops 40960 | bytes 262149 | tf_op jit(solution)/shard_map/while/body/jit(dynamic_update_index_in_dim)/dynamic_update_slice | solution.py:103
  93.7 1.4 %bitcast_dynamic-update-slice_fusion.17 = (f32[8,64,128]{2,1,0:T(8,128)}, f32[64,128]{1,0:T(8,128)S(1)}, f32[8,64,128]{2,1,0:T(8,128)}) fusion(f32[8,64,128]{2,1,0:T(8,128)} %get-tuple-element.1346, s32[]{:T(128)S(6)} %sub.273, f32[64,128]{1,0:T(8,128)S(1)} %get-tuple-element.1345, pred[]{:T(512)S(6)} %compare.143, ...), kind=kLoop, calls=%fused_computation.18.clone.1 | loop fusion | flops 40960 | bytes 262149 | tf_op jit(solution)/shard_map/while/body/jit(dynamic_update_index_in_dim)/dynamic_update_slice | solution.py:103
  95.2 1.5 %bitcast_dynamic-update-slice_fusion.17 = (f32[8,64,128]{2,1,0:T(8,128)}, f32[64,128]{1,0:T(8,128)S(1)}, f32[8,64,128]{2,1,0:T(8,128)}) fusion(f32[8,64,128]{2,1,0:T(8,128)} %get-tuple-element.1346, s32[]{:T(128)S(6)} %sub.273, f32[64,128]{1,0:T(8,128)S(1)} %get-tuple-element.1345, pred[]{:T(512)S(6)} %compare.143, ...), kind=kLoop, calls=%fused_computation.18.clone.1 | loop fusion | flops 40960 | bytes 262149 | tf_op jit(solution)/shard_map/while/body/jit(dynamic_update_index_in_dim)/dynamic_update_slice | solution.py:103
  96.6 1.4 %bitcast_dynamic-update-slice_fusion.17 = (f32[8,64,128]{2,1,0:T(8,128)}, f32[64,128]{1,0:T(8,128)S(1)}, f32[8,64,128]{2,1,0:T(8,128)}) fusion(f32[8,64,128]{2,1,0:T(8,128)} %get-tuple-element.1346, s32[]{:T(128)S(6)} %sub.273, f32[64,128]{1,0:T(8,128)S(1)} %get-tuple-element.1345, pred[]{:T(512)S(6)} %compare.143, ...), kind=kLoop, calls=%fused_computation.18.clone.1 | loop fusion | flops 40960 | bytes 262149 | tf_op jit(solution)/shard_map/while/body/jit(dynamic_update_index_in_dim)/dynamic_update_slice | solution.py:103
  98.1 1.5 %bitcast_dynamic-update-slice_fusion.17 = (f32[8,64,128]{2,1,0:T(8,128)}, f32[64,128]{1,0:T(8,128)S(1)}, f32[8,64,128]{2,1,0:T(8,128)}) fusion(f32[8,64,128]{2,1,0:T(8,128)} %get-tuple-element.1346, s32[]{:T(128)S(6)} %sub.273, f32[64,128]{1,0:T(8,128)S(1)} %get-tuple-element.1345, pred[]{:T(512)S(6)} %compare.143, ...), kind=kLoop, calls=%fused_computation.18.clone.1 | loop fusion | flops 40960 | bytes 262149 | tf_op jit(solution)/shard_map/while/body/jit(dynamic_update_index_in_dim)/dynamic_update_slice | solution.py:103
  103.3 2.1 %multiply_add_fusion.24 = (f32[64,16,128]{2,0,1:T(8,128)S(1)}, f32[64,16,128]{2,0,1:T(8,128)S(1)}, f32[64,16,128]{2,0,1:T(8,128)S(1)}, f32[64,16,128]{2,0,1:T(8,...) fusion(f32[64,16,128]{2,0,1:T(8,128)S(1)} %copy-done.5, ...), kind=kLoop, calls=%fused_computation.141 | loop fusion | flops 2359296 | bytes 11476992 | tf_op jit(solution)/shard_map/add | solution.py:56
  121.5 13.8 %all-gather.1 = f32[24,64,16]{1,2,0:T(8,128)S(1)} all-gather(f32[6,64,16]{1,2,0:T(8,128)S(1)} %constant_dynamic-update-slice_fusion), channel_id=3, replica_groups=mesh['row'=8,'col'=4] {'col'}, dimensions={0}, use_global_device_ids=true | all-gather | bytes 122880 | tf_op jit(solution)/shard_map/all_gather | solution.py:165
  (202 shorter events, 54.5 us)
Async XLA Ops:
  6.5 62.6 %all-gather.4.cloned.1.call-start = ((), (), s32[]{:S(2)}) async-start(), calls=%async_computation | async-start | bytes 1769472 | tf_op jit(solution)/shard_map/all_gather | solution.py:152
  9.1 4.4 %collective-permute-start.1 = (f32[2,64,1,128]{3,1,2,0:T(8,128)S(1)}, f32[2,64,1,128]{3,1,2,0:T(8,128)S(1)}, u32[]{:S(2)}, u32[]{:S(2)}) collective-permute-start(f32[2,64,1,128]{3,1,2,0:T(8,128)S(1)} %get-tuple-element.851), channel_id=1, source_target_pairs={{4,0},{8,4},{12,8},{16,12},{20,16},{24,20},{28,24},{5,1},{9,5},{13... | collective-permute-start | bytes 196616 | tf_op jit(solution)/shard_map/ppermute | solution.py:17
  10.4 3.9 %collective-permute-start = (f32[2,64,1,128]{3,1,2,0:T(8,128)S(1)}, f32[2,64,1,128]{3,1,2,0:T(8,128)S(1)}, u32[]{:S(2)}, u32[]{:S(2)}) collective-permute-start(f32[2,64,1,128]{3,1,2,0:T(8,128)S(1)} %get-tuple-element.850), channel_id=1, source_target_pairs={{0,4},{4,8},{8,12},{12,16},{16,20},{20,24},{24,28},{1,5},{5,9},{9,... | collective-permute-start | bytes 196616 | tf_op jit(solution)/shard_map/ppermute | solution.py:14
  15.9 7.9 %collective-permute-start.3 = (f32[2,64,18,1]{1,0,3,2:T(2,128)}, f32[2,64,18,1]{1,0,3,2:T(2,128)S(1)}, u32[]{:S(2)}, u32[]{:S(2)}) collective-permute-start(f32[2,64,18,1]{1,0,3,2:T(2,128)} %copy.304), channel_id=1, source_target_pairs={{1,0},{2,1},{3,2},{5,4},{6,5},{7,6},{9,8},{10,9},{11,10},{13,12},{... | collective-permute-start | bytes 27656 | tf_op jit(solution)/shard_map/ppermute | solution.py:17
  17.6 7.0 %collective-permute-start.2 = (f32[2,64,18,1]{1,0,3,2:T(2,128)S(1)}, f32[2,64,18,1]{1,0,3,2:T(2,128)}, u32[]{:S(2)}, u32[]{:S(2)}) collective-permute-start(f32[2,64,18,1]{1,0,3,2:T(2,128)S(1)} %copy.303), channel_id=1, source_target_pairs={{0,1},{1,2},{2,3},{4,5},{5,6},{6,7},{8,9},{9,10},{10,11},{12,13},{... | collective-permute-start | bytes 27656 | tf_op jit(solution)/shard_map/ppermute | solution.py:14
  26.8 1.0 copy-start
  26.8 1.2 copy-start.19
  26.8 1.3 copy-start.20
  36.0 1.0 copy-start.10
  38.0 1.0 copy-start.1
  39.8 4.5 %copy-start.2 = (f32[64,16,128]{2,0,1:T(8,128)}, f32[64,16,128]{2,0,1:T(8,128)S(1)}, u32[]{:S(2)}) copy-start(f32[64,16,128]{2,0,1:T(8,128)S(1)} %get-tuple-element.745) | copy-start | bytes 1572868
  39.8 4.5 %copy-start.4 = (f32[64,16,128]{2,0,1:T(8,128)}, f32[64,16,128]{2,0,1:T(8,128)S(1)}, u32[]{:S(2)}) copy-start(f32[64,16,128]{2,0,1:T(8,128)S(1)} %get-tuple-element.747) | copy-start | bytes 1572868
  73.7 27.4 %copy-start.11 = (f32[64,16,128]{2,0,1:T(8,128)S(1)}, f32[64,16,128]{2,0,1:T(8,128)}, u32[]{:S(2)}) copy-start(f32[64,16,128]{2,0,1:T(8,128)} %copy-done.10) | copy-start | bytes 1572868
  74.4 26.7 %copy-start.9 = (f32[64,16,128]{2,0,1:T(8,128)S(1)}, f32[64,16,128]{2,0,1:T(8,128)}, u32[]{:S(2)}) copy-start(f32[64,16,128]{2,0,1:T(8,128)} %copy-done.8) | copy-start | bytes 1572868
  86.5 14.6 %copy-start.7 = (f32[64,16,128]{2,0,1:T(8,128)S(1)}, f32[64,16,128]{2,0,1:T(8,128)}, u32[]{:S(2)}) copy-start(f32[64,16,128]{2,0,1:T(8,128)} %copy-done.6) | copy-start | bytes 1572868
  101.1 1.0 copy-start.15
  101.1 1.2 copy-start.16
  101.1 1.3 copy-start.17
  101.1 1.5 %copy-start.18 = (f32[64,16,127]{2,0,1:T(8,128)S(1)}, f32[64,16,127]{2,0,1:T(8,128)}, u32[]{:S(2)}) copy-start(f32[64,16,127]{2,0,1:T(8,128)} %get-tuple-element.972) | copy-start | bytes 1560580
  101.2 1.5 %copy-start.3 = (f32[64,16,128]{2,0,1:T(8,128)S(1)}, f32[64,16,128]{2,0,1:T(8,128)}, u32[]{:S(2)}) copy-start(f32[64,16,128]{2,0,1:T(8,128)} %copy-done.2) | copy-start | bytes 1572868
  101.2 1.7 %copy-start.5 = (f32[64,16,128]{2,0,1:T(8,128)S(1)}, f32[64,16,128]{2,0,1:T(8,128)}, u32[]{:S(2)}) copy-start(f32[64,16,128]{2,0,1:T(8,128)} %copy-done.4) | copy-start | bytes 1572868
  101.3 1.8 %copy-start.13 = (f32[64,16,127]{2,0,1:T(8,128)S(1)}, f32[64,16,127]{2,0,1:T(8,128)}, u32[]{:S(2)}) copy-start(f32[64,16,127]{2,0,1:T(8,128)} %get-tuple-element.938) | copy-start | bytes 1560580
  101.3 2.0 %copy-start.14 = (f32[64,16,127]{2,0,1:T(8,128)S(1)}, f32[64,16,127]{2,0,1:T(8,128)}, u32[]{:S(2)}) copy-start(f32[64,16,127]{2,0,1:T(8,128)} %get-tuple-element.939) | copy-start | bytes 1560580
  121.5 14.4 %copy-start.12 = (f32[64,16,128]{2,1,0:T(8,128)S(1)}, f32[64,16,128]{2,1,0:T(8,128)}, u32[]{:S(2)}) copy-start(f32[64,16,128]{2,1,0:T(8,128)} %param.10) | copy-start | bytes 1572868
  (3 other events, 2.3 us)
Sparse Core Ops, SparseCore 0:
  37.9 31.1 all-gather.3
where the time goes:
time: 146 us; the launch traced here: 144 us
  other arithmetic  43.1 us (30%)
  local copies, waits for them, and re-layouts  36.4 us (25%)
  waiting for transfers between devices  24.6 us (17%)
  between operations  14.2 us (10%)
  blocking collectives  13.8 us (9%)
  starting transfers between devices  11.8 us (8%)
    dynamic_update_slice x24, other arithmetic, join_spikes(): unused, outputs = lax.scan(forward, (zero_plane, zero_plane), columns_in)  23.8 us
    all_gather x1, waiting for transfers between devices, on_device(): gathered = lax.all_gather(planes, 'row', axis=0, tiled=True)  23.3 us
    all_gather x1, blocking collectives, on_device(): gathered = lax.all_gather(planes, 'col', axis=0, tiled=True)  13.8 us
    add x11, other arithmetic, reduce_lines(): column + left_factor * shifted(column, line_axis, stride, 0.0)  10.7 us
    slice x41, local copies, waits for them, and re-layouts, shifted(): kept_part = lax.slice_in_dim(values, 0, length - stride, axis=line_axis)  9.44 us
    ppermute x2, starting transfers between devices, padded_2(): lax.ppermute(lax.slice_in_dim(block, block.shape[dim] - width, None, axis...  9.22 us
    unnamed x55, local copies, waits for them, and re-layouts  8.25 us
    slice x24, local copies, waits for them, and re-layouts, shifted(): kept_part = lax.slice_in_dim(values, -stride, length, axis=line_axis)  5.6 us
  transfers between devices with their start and end apart: 5, of which 3 were waited for; matrix products, arithmetic and copies ran while one was open for 6% of the time, Pallas kernels for 0%

commit v1 on v0

--- a/solution.py
+++ b/solution.py
@@ -162,7 +162,28 @@
     local_part, left_spike, right_spike, planes = local_spikes(
         -west_ydir, -east_ydir, delta_xdir, 2
     )
-    gathered = lax.all_gather(planes, "col", axis=0, tiled=True)
+
+    def _see_cells(u_in, array_axis):
+        link_axis = "col"
+        world_n = lax.psum(1, link_axis)
+        r1 = range(world_n)
+        all_rows = map(lambda q: (q, (q + 1) % world_n), r1)
+        trail = list(all_rows)
+
+        def state_sheet_for(block_out):
+            if len(block_out) == world_n:
+                return block_out
+            built = lax.ppermute(block_out[0], perm=trail, axis_name=link_axis)
+            prior = state_sheet_for([built, *block_out])
+            return prior
+
+        latest = state_sheet_for([u_in])
+        newest = jnp.concatenate(latest, array_axis)
+        y_new = lax.axis_index(link_axis)
+        step_out = jnp.roll(newest, (y_new + 1) * u_in.shape[array_axis], axis=array_axis)
+        return step_out
+
+    gathered = _see_cells(planes, 0)
     delta_ydir = join_spikes(
         gathered,
         local_part,

time: 146 us -> 150 us (1.027)
  waiting for transfers between devices: 24.6 us -> 40.9 us
  blocking collectives: 13.8 us -> 0 us
  starting transfers between devices: 11.8 us -> 13.3 us
    ppermute x0 -> x3, waiting for transfers between devices: none -> 16.2 us  [state_sheet_for(): built = lax.ppermute(block_out[0], perm=trail, axis_name=link_axis)]
    all_gather x1 -> x0, blocking collectives: 13.8 us -> none  [on_device(): gathered = lax.all_gather(planes, 'col', axis=0, tiled=True)]
    ppermute x0 -> x3, starting transfers between devices: none -> 1.54 us  [state_sheet_for(): built = lax.ppermute(block_out[0], perm=trail, axis_name=link_axis)]
    unnamed x55 -> x62, local copies, waits for them, and re-layouts: 8.25 us -> 8.75 us
  transfers between devices with their start and end apart: 5 -> 8, of which waited for: 3 -> 6; matrix products, arithmetic and copies ran while one was open for 6% -> 5% of each run, Pallas kernels for 0% -> 0%
where the time goes in v1:
time: 150 us; the launch traced here: 148 us
  other arithmetic  42.8 us (29%)
  waiting for transfers between devices  40.9 us (27%)
  local copies, waits for them, and re-layouts  36.8 us (25%)
  between operations  14.3 us (10%)
  starting transfers between devices  13.3 us (9%)
    dynamic_update_slice x24, other arithmetic, join_spikes(): unused, outputs = lax.scan(forward, (zero_plane, zero_plane), columns_in)  23.5 us
    all_gather x1, waiting for transfers between devices, on_device(): gathered = lax.all_gather(planes, 'row', axis=0, tiled=True)  23.4 us
    ppermute x3, waiting for transfers between devices, state_sheet_for(): built = lax.ppermute(block_out[0], perm=trail, axis_name=link_axis)  16.2 us
    add x11, other arithmetic, reduce_lines(): column + left_factor * shifted(column, line_axis, stride, 0.0)  10.7 us
    slice x41, local copies, waits for them, and re-layouts, shifted(): kept_part = lax.slice_in_dim(values, 0, length - stride, axis=line_axis)  9.37 us
    ppermute x2, starting transfers between devices, padded_2(): lax.ppermute(lax.slice_in_dim(block, block.shape[dim] - width, None, axis...  9.22 us
    unnamed x62, local copies, waits for them, and re-layouts  8.75 us
    slice x24, local copies, waits for them, and re-layouts, shifted(): kept_part = lax.slice_in_dim(values, -stride, length, axis=line_axis)  5.57 us
  transfers between devices with their start and end apart: 8, of which 6 were waited for; matrix products, arithmetic and copies ran while one was open for 5% of the time, Pallas kernels for 0%

profile of v1, /device:TPU:0, one launch (start us, length us, event | category | flops | bytes accessed | tf_op | source)
XLA Modules:
  0.0 148.4 jit_solution(16717474656156676164)
XLA Ops:
  6.5 2.5 %fusion.53 = (f32[64,16,128]{2,0,1:T(8,128)}, f32[1,64,16,128]{3,1,2,0:T(8,128)S(1)}, f32[1,64,16,128]{3,1,2,0:T(8,128)S(1)}, f32[64,16,128]{2,0,1:T(8,128)}) fusion(f32[64,16,128]{2,1,0:T(8,128)} %param.10, f32[64,16,128]{2,1,0:T(8,128)} %param.11), kind=kLoop, calls=%fused_computation.249 | loop fusion | bytes 3145728 | tf_op args[0]
  10.4 3.0 %collective-permute-start = (f32[2,64,1,128]{3,1,2,0:T(8,128)S(1)}, f32[2,64,1,128]{3,1,2,0:T(8,128)S(1)}, u32[]{:S(2)}, u32[]{:S(2)}) collective-permute-start(f32[2,64,1,128]{3,1,2,0:T(8,128)S(1)} %get-tuple-element.863), channel_id=1, source_target_pairs={{0,4},{4,8},{8,12},{12,16},{16,20},{20,24},{24,28},{1,5},{5,9},{9,... | collective-permute-start | bytes 196616 | tf_op jit(solution)/shard_map/ppermute | solution.py:14
  17.6 6.2 %collective-permute-start.2 = (f32[2,64,18,1]{1,0,3,2:T(2,128)S(1)}, f32[2,64,18,1]{1,0,3,2:T(2,128)}, u32[]{:S(2)}, u32[]{:S(2)}) collective-permute-start(f32[2,64,18,1]{1,0,3,2:T(2,128)S(1)} %copy.267), channel_id=1, source_target_pairs={{0,1},{1,2},{2,3},{4,5},{5,6},{6,7},{8,9},{9,10},{10,11},{12,13},{... | collective-permute-start | bytes 27656 | tf_op jit(solution)/shard_map/ppermute | solution.py:14
  45.6 23.4 %all-gather.3.cloned.1.call-done = f32[48,64,128]{2,1,0:T(8,128)} async-done(((f32[6,64,128]{2,1,0:T(8,128)}), f32[48,64,128]{2,1,0:T(8,128)}) %all-gather.3.cloned.1.call-update) | async-done | bytes 1572880 | tf_op jit(solution)/shard_map/all_gather | solution.py:152
  69.1 2.4 %slice_bitcast_fusion.2 = (f32[8,64,128]{2,1,0:T(8,128)S(1)}, f32[8,64,128]{2,1,0:T(8,128)S(1)}, f32[8,64,128]{2,1,0:T(8,128)}, f32[8,64,128]{2,1,0:T(8,128)}, f32[8,64,128]{2,1,0:T(8,128)}, /*index=5*/f32[8,64,128]{2,1,0:T(8,128)}) fusion(f32[8,6,64,128]{3,2,1,0:T(8,128)} %bitcast.271), kind=kLoop, calls=%fused_computation.177 | loop fusion | bytes 3145728 | tf_op jit(solution)/shard_map/squeeze | solution.py:90
  74.4 11.9 %while.80 = (s32[]{:T(128)}, f32[64,128]{1,0:T(8,128)S(1)}, f32[64,128]{1,0:T(8,128)S(1)}, f32[8,64,128]{2,1,0:T(8,128)}, f32[8,64,128]{2,1,0:T(8,128)}, /*index...) while((s32[]{:T(128)}, f32[64,128]{1,0:T(8,128)S(1)}, ...), condition=%wide.region_1.2_spmd.clone, body=%wide.region_0.1_spmd.clone.sunk | while | flops 122883 | bytes 458915 | solution.py:103
  74.4 1.6 %bitcast_dynamic-update-slice_fusion.16 = (f32[8,64,128]{2,1,0:T(8,128)}, f32[64,128]{1,0:T(8,128)S(1)}, f32[8,64,128]{2,1,0:T(8,128)}, f32[8,64,128]{2,1,0:T(8,...) fusion(f32[8,64,128]{2,1,0:T(8,128)} %get-tuple-element.1322, s32[]{:T(128)S(6)} %copy.360, ...), kind=kLoop, calls=%fused_computation.clone.1 | loop fusion | flops 122880 | bytes 458757 | tf_op jit(solution)/shard_map/while/body/jit(dynamic_update_index_in_dim)/dynamic_update_slice | solution.py:103
  75.9 1.5 bitcast_dynamic-update-slice_fusion.16
  77.4 1.5 bitcast_dynamic-update-slice_fusion.16
  78.9 1.5 bitcast_dynamic-update-slice_fusion.16
  80.3 1.5 bitcast_dynamic-update-slice_fusion.16
  81.8 1.5 bitcast_dynamic-update-slice_fusion.16
  83.3 1.5 %bitcast_dynamic-update-slice_fusion.16 = (f32[8,64,128]{2,1,0:T(8,128)}, f32[64,128]{1,0:T(8,128)S(1)}, f32[8,64,128]{2,1,0:T(8,128)}, f32[8,64,128]{2,1,0:T(8,...) fusion(f32[8,64,128]{2,1,0:T(8,128)} %get-tuple-element.1322, s32[]{:T(128)S(6)} %copy.360, ...), kind=kLoop, calls=%fused_computation.clone.1 | loop fusion | flops 122880 | bytes 458757 | tf_op jit(solution)/shard_map/while/body/jit(dynamic_update_index_in_dim)/dynamic_update_slice | solution.py:103
  84.8 1.5 bitcast_dynamic-update-slice_fusion.16
  87.7 11.5 %while.81 = (s32[]{:T(128)}, f32[64,128]{1,0:T(8,128)S(1)}, f32[8,64,128]{2,1,0:T(8,128)}, f32[8,64,128]{2,1,0:T(8,128)}, f32[8,64,128]{2,1,0:T(8,128)}, /*index...) while((s32[]{:T(128)}, f32[64,128]{1,0:T(8,128)S(1)}, ...), condition=%wide.region_3.4_spmd.clone, body=%wide.region_2.3_spmd.clone.sunk | while | flops 40964 | bytes 262287 | solution.py:111
  89.2 1.5 bitcast_dynamic-update-slice_fusion.17
  90.6 1.4 bitcast_dynamic-update-slice_fusion.17
  92.1 1.4 bitcast_dynamic-update-slice_fusion.17
  94.9 1.4 bitcast_dynamic-update-slice_fusion.17
  103.0 2.1 %multiply_add_fusion.24 = (f32[64,16,128]{2,0,1:T(8,128)S(1)}, f32[64,16,128]{2,0,1:T(8,128)S(1)}, f32[64,16,128]{2,0,1:T(8,128)S(1)}, f32[64,16,128]{2,0,1:T(8,...) fusion(f32[64,16,128]{2,0,1:T(8,128)S(1)} %copy-done.5, ...), kind=kLoop, calls=%fused_computation.141 | loop fusion | flops 2359296 | bytes 11476992 | tf_op jit(solution)/shard_map/add | solution.py:56
  121.2 1.5 %collective-permute-start.4 = (f32[1,6,64,16]{2,3,1,0:T(8,128)S(1)}, f32[1,6,64,16]{2,3,1,0:T(8,128)S(1)}, u32[]{:S(2)}, u32[]{:S(2)}) collective-permute-start(f32[1,6,64,16]{2,3,1,0:T(8,128)S(1)} %bitcast.272), channel_id=1, source_target_pairs={{0,1},{1,2},{2,3},{3,0},{4,5},{5,6},{6,7},{7,4},{8,9},{9,10},{10,1... | collective-permute-start | bytes 73736 | tf_op jit(solution)/shard_map/ppermute | solution.py:176
  122.8 4.4 %collective-permute-done.4 = f32[1,6,64,16]{2,3,1,0:T(8,128)S(1)} collective-permute-done((f32[1,6,64,16]{2,3,1,0:T(8,128)S(1)}, f32[1,6,64,16]{2,3,1,0:T(8,128)S(1)}, u32[]{:S(2)}, u32[]{:S(2)}) %collective-permute-start.4) | collective-permute-done | bytes 24608 | tf_op jit(solution)/shard_map/ppermute | solution.py:176
  127.2 5.9 %collective-permute-done.5 = f32[1,6,64,16]{2,3,1,0:T(8,128)S(1)} collective-permute-done((f32[1,6,64,16]{2,3,1,0:T(8,128)S(1)}, f32[1,6,64,16]{2,3,1,0:T(8,128)S(1)}, u32[]{:S(2)}, u32[]{:S(2)}) %collective-permute-start.5) | collective-permute-done | bytes 24608 | tf_op jit(solution)/shard_map/ppermute | solution.py:176
  133.1 5.9 %collective-permute-done.6 = f32[1,6,64,16]{2,3,1,0:T(8,128)S(1)} collective-permute-done((f32[1,6,64,16]{2,3,1,0:T(8,128)S(1)}, f32[1,6,64,16]{2,3,1,0:T(8,128)S(1)}, u32[]{:S(2)}, u32[]{:S(2)}) %collective-permute-start.6) | collective-permute-done | bytes 24608 | tf_op jit(solution)/shard_map/ppermute | solution.py:176
  (215 shorter events, 59.2 us)
Async XLA Ops:
  6.5 62.5 %all-gather.3.cloned.1.call-start = ((), (), s32[]{:S(2)}) async-start(), calls=%async_computation | async-start | bytes 1769472 | tf_op jit(solution)/shard_map/all_gather | solution.py:152
  9.1 4.4 %collective-permute-start.1 = (f32[2,64,1,128]{3,1,2,0:T(8,128)S(1)}, f32[2,64,1,128]{3,1,2,0:T(8,128)S(1)}, u32[]{:S(2)}, u32[]{:S(2)}) collective-permute-start(f32[2,64,1,128]{3,1,2,0:T(8,128)S(1)} %get-tuple-element.864), channel_id=1, source_target_pairs={{4,0},{8,4},{12,8},{16,12},{20,16},{24,20},{28,24},{5,1},{9,5},{13... | collective-permute-start | bytes 196616 | tf_op jit(solution)/shard_map/ppermute | solution.py:17
  10.4 3.9 %collective-permute-start = (f32[2,64,1,128]{3,1,2,0:T(8,128)S(1)}, f32[2,64,1,128]{3,1,2,0:T(8,128)S(1)}, u32[]{:S(2)}, u32[]{:S(2)}) collective-permute-start(f32[2,64,1,128]{3,1,2,0:T(8,128)S(1)} %get-tuple-element.863), channel_id=1, source_target_pairs={{0,4},{4,8},{8,12},{12,16},{16,20},{20,24},{24,28},{1,5},{5,9},{9,... | collective-permute-start | bytes 196616 | tf_op jit(solution)/shard_map/ppermute | solution.py:14
  15.9 7.9 %collective-permute-start.3 = (f32[2,64,18,1]{1,0,3,2:T(2,128)}, f32[2,64,18,1]{1,0,3,2:T(2,128)S(1)}, u32[]{:S(2)}, u32[]{:S(2)}) collective-permute-start(f32[2,64,18,1]{1,0,3,2:T(2,128)} %copy.268), channel_id=1, source_target_pairs={{1,0},{2,1},{3,2},{5,4},{6,5},{7,6},{9,8},{10,9},{11,10},{13,12},{... | collective-permute-start | bytes 27656 | tf_op jit(solution)/shard_map/ppermute | solution.py:17
  17.6 7.0 %collective-permute-start.2 = (f32[2,64,18,1]{1,0,3,2:T(2,128)S(1)}, f32[2,64,18,1]{1,0,3,2:T(2,128)}, u32[]{:S(2)}, u32[]{:S(2)}) collective-permute-start(f32[2,64,18,1]{1,0,3,2:T(2,128)S(1)} %copy.267), channel_id=1, source_target_pairs={{0,1},{1,2},{2,3},{4,5},{5,6},{6,7},{8,9},{9,10},{10,11},{12,13},{... | collective-permute-start | bytes 27656 | tf_op jit(solution)/shard_map/ppermute | solution.py:14
  26.8 1.0 copy-start
  26.8 1.2 copy-start.19
  26.8 1.3 copy-start.20
  38.0 1.0 copy-start.1
  39.7 4.4 %copy-start.2 = (f32[64,16,128]{2,0,1:T(8,128)}, f32[64,16,128]{2,0,1:T(8,128)S(1)}, u32[]{:S(2)}) copy-start(f32[64,16,128]{2,0,1:T(8,128)S(1)} %get-tuple-element.758) | copy-start | bytes 1572868
  39.7 4.4 %copy-start.4 = (f32[64,16,128]{2,0,1:T(8,128)}, f32[64,16,128]{2,0,1:T(8,128)S(1)}, u32[]{:S(2)}) copy-start(f32[64,16,128]{2,0,1:T(8,128)S(1)} %get-tuple-element.760) | copy-start | bytes 1572868
  73.7 27.1 %copy-start.11 = (f32[64,16,128]{2,0,1:T(8,128)S(1)}, f32[64,16,128]{2,0,1:T(8,128)}, u32[]{:S(2)}) copy-start(f32[64,16,128]{2,0,1:T(8,128)} %copy-done.10) | copy-start | bytes 1572868
  74.4 26.4 %copy-start.9 = (f32[64,16,128]{2,0,1:T(8,128)S(1)}, f32[64,16,128]{2,0,1:T(8,128)}, u32[]{:S(2)}) copy-start(f32[64,16,128]{2,0,1:T(8,128)} %copy-done.8) | copy-start | bytes 1572868
  86.3 14.5 %copy-start.7 = (f32[64,16,128]{2,0,1:T(8,128)S(1)}, f32[64,16,128]{2,0,1:T(8,128)}, u32[]{:S(2)}) copy-start(f32[64,16,128]{2,0,1:T(8,128)} %copy-done.6) | copy-start | bytes 1572868
  100.8 1.2 copy-start.16
  100.8 1.3 copy-start.17
  100.8 1.5 %copy-start.18 = (f32[64,16,127]{2,0,1:T(8,128)S(1)}, f32[64,16,127]{2,0,1:T(8,128)}, u32[]{:S(2)}) copy-start(f32[64,16,127]{2,0,1:T(8,128)} %get-tuple-element.985) | copy-start | bytes 1560580
  101.0 1.5 %copy-start.3 = (f32[64,16,128]{2,0,1:T(8,128)S(1)}, f32[64,16,128]{2,0,1:T(8,128)}, u32[]{:S(2)}) copy-start(f32[64,16,128]{2,0,1:T(8,128)} %copy-done.2) | copy-start | bytes 1572868
  101.0 1.7 %copy-start.5 = (f32[64,16,128]{2,0,1:T(8,128)S(1)}, f32[64,16,128]{2,0,1:T(8,128)}, u32[]{:S(2)}) copy-start(f32[64,16,128]{2,0,1:T(8,128)} %copy-done.4) | copy-start | bytes 1572868
  101.0 1.8 %copy-start.13 = (f32[64,16,127]{2,0,1:T(8,128)S(1)}, f32[64,16,127]{2,0,1:T(8,128)}, u32[]{:S(2)}) copy-start(f32[64,16,127]{2,0,1:T(8,128)} %get-tuple-element.951) | copy-start | bytes 1560580
  101.0 2.0 %copy-start.14 = (f32[64,16,127]{2,0,1:T(8,128)S(1)}, f32[64,16,127]{2,0,1:T(8,128)}, u32[]{:S(2)}) copy-start(f32[64,16,127]{2,0,1:T(8,128)} %get-tuple-element.952) | copy-start | bytes 1560580
  121.2 5.9 %collective-permute-start.4 = (f32[1,6,64,16]{2,3,1,0:T(8,128)S(1)}, f32[1,6,64,16]{2,3,1,0:T(8,128)S(1)}, u32[]{:S(2)}, u32[]{:S(2)}) collective-permute-start(f32[1,6,64,16]{2,3,1,0:T(8,128)S(1)} %bitcast.272), channel_id=1, source_target_pairs={{0,1},{1,2},{2,3},{3,0},{4,5},{5,6},{6,7},{7,4},{8,9},{9,10},{10,1... | collective-permute-start | bytes 73736 | tf_op jit(solution)/shard_map/ppermute | solution.py:176
  127.2 5.9 %collective-permute-start.5 = (f32[1,6,64,16]{2,3,1,0:T(8,128)S(1)}, f32[1,6,64,16]{2,3,1,0:T(8,128)S(1)}, u32[]{:S(2)}, u32[]{:S(2)}) collective-permute-start(f32[1,6,64,16]{2,3,1,0:T(8,128)S(1)} %collective-permute-done.4), channel_id=1, source_target_pairs={{0,1},{1,2},{2,3},{3,0},{4,5},{5,6},{6,7},{7,4},{8,9},{9,10},{10,1... | collective-permute-start | bytes 73736 | tf_op jit(solution)/shard_map/ppermute | solution.py:176
  133.1 5.9 %collective-permute-start.6 = (f32[1,6,64,16]{2,3,1,0:T(8,128)S(1)}, f32[1,6,64,16]{2,3,1,0:T(8,128)S(1)}, u32[]{:S(2)}, u32[]{:S(2)}) collective-permute-start(f32[1,6,64,16]{2,3,1,0:T(8,128)S(1)} %collective-permute-done.5), channel_id=1, source_target_pairs={{0,1},{1,2},{2,3},{3,0},{4,5},{5,6},{6,7},{7,4},{8,9},{9,10},{10,1... | collective-permute-start | bytes 73736 | tf_op jit(solution)/shard_map/ppermute | solution.py:176
  (6 other events, 5.3 us)
Sparse Core Ops, SparseCore 0:
  37.8 31.1 all-gather.2
